TPU v7x, 32 devices: a whole 2x2x4 slice. The times are simulated.
32 devices in a mesh: prow: 4 (over y, core), pcol: 8 (over z, x).
Axes of the slice: x: 2, y: 2, z: 4, core: 2. Of those that a mesh axis runs over, the one named last changes fastest.
Arguments:
- vectors: bfloat16 [512, 120064], P('pcol', 'prow'), may hold values from -6 to 6
- reflectors: bfloat16 [2, 256, 120064], P(None, 'pcol', 'prow'), may hold values from -6 to 6
- panel_factor: float32 [2, 256, 256], replicated, as said below
Outputs:
- band_vectors: bfloat16 [8, 64, 120064], P('pcol', 'prow')
Inputs may be any that keep to these rules, and one draw needn't show every extreme that they name: `panel_factor`: upper triangular: zero below the diagonal; diagonal entries between 1 / 120064 and 3 / 120064.
All inputs are finite; a program needn't handle non-finite values.
Results may differ from a plain program's by a relative error of at most 0.0095.
Values may be sent and summed in bfloat16 or wider, within the bound.
No kernel may reach another device: no remote copies, remote signals or barrier semaphores. Data moves between devices by JAX's collectives and lax.ppermute only.
A program may use at most 192 MiB of HBM per device.

v0:
```python
import jax
import jax.numpy as jnp
from jax import lax
from jax.sharding import PartitionSpec as P


def finish_panel(current, panel, factor, projected):
    scaled = lax.dot_general(
        projected,
        factor,
        (((1,), (1,)), ((), ())),
        precision=lax.Precision.HIGHEST,
        preferred_element_type=jnp.float32,
    ).astype(jnp.bfloat16)
    updated = current.astype(jnp.float32) - jnp.dot(
        scaled, panel, preferred_element_type=jnp.float32
    )
    return updated.astype(jnp.bfloat16)


def partial_products(current, panel):
    return lax.dot_general(
        current, panel, (((1,), (1,)), ((), ())), preferred_element_type=jnp.float32
    )


def apply_panel(current, panel, factor):
    partial_sum = partial_products(current, panel)
    projected = lax.psum(partial_sum.astype(jnp.bfloat16), "prow").astype(jnp.float32)
    return finish_panel(current, panel, factor, projected)


def body(vectors, reflectors, panel_factor):
    current = vectors
    for number in range(reflectors.shape[0]):
        single = lax.all_gather(reflectors[number], "pcol", axis=0, tiled=True)
        current = apply_panel(current, single, panel_factor[number])
    owned_rows = lax.all_to_all(current, "prow", split_axis=0, concat_axis=1, tiled=True)
    return owned_rows[None]


def solution(mesh):
    placed = (P("pcol", "prow"), P(None, "pcol", "prow"), P())
    return jax.shard_map(
        body, mesh=mesh, in_specs=placed, out_specs=P("pcol", "prow", None), check_vma=False
    )
```

profile of v0, /device:TPU:0, one launch (start us, length us, event | category | flops | bytes accessed | tf_op | source)
XLA Modules:
  0.0 529.0 jit_solution(264437417981960315)
XLA Ops:
  6.5 0.0 all-gather.5.cloned.1.call-start
  6.5 4.2 fusion.18
  10.8 0.0 all-gather.5.cloned.1.call-update
  10.8 0.0 all-gather.7.cloned.1.call-start
  10.9 0.7 all-gather.7.cloned.1.call-update
  11.6 0.0 copy-start
  11.6 212.6 %all-gather.5.cloned.1.call-done = bf16[1,256,30016]{2,1,0:T(8,128)(2,1)} async-done(((bf16[1,32,30016]{2,1,0:T(8,128)(2,1)}), bf16[1,256,30016]{2,1,0:T(8,128)(2,1)}) %all-gather.5.cloned.1.call-update) | async-done | bytes 15368208 | tf_op jit(solution)/shard_map/all_gather | solution.py:36
  224.2 11.2 %fusion.8 = bf16[64,256]{1,0:T(8,128)(2,1)S(1)} fusion(bf16[64,30016]{1,0:T(8,128)(2,1)} %param.3, bf16[1,256,30016]{2,1,0:T(8,128)(2,1)} %all-gather.5.cloned.1.call-done), kind=kOutput, calls=%fused_computation.10 | convolution fusion | flops 983580672 | bytes 19243008 | tf_op jit(solution)/shard_map/dot_general | solution.py:22
  235.4 11.2 %psum.14 = bf16[64,256]{1,0:T(8,128)(2,1)S(1)} all-reduce(bf16[64,256]{1,0:T(8,128)(2,1)S(1)} %fusion.8), channel_id=1, replica_groups=mesh['prow'=4,'pcol'=8] {'prow'}, use_global_device_ids=true, to_apply=%region_0.0 | all-reduce | flops 16384 | bytes 65536 | tf_op jit(solution)/shard_map/psum | solution.py:29
  246.6 0.0 copy-done
  246.6 0.3 convolution_convert_fusion.1
  246.9 10.6 %fusion = bf16[64,30016]{1,0:T(8,128)(2,1)} fusion(bf16[64,256]{1,0:T(8,128)(2,1)S(1)} %convolution_convert_fusion.1, bf16[1,256,30016]{2,1,0:T(8,128)(2,1)} %all-gather.5.cloned.1.call-done, bf16[64,30016]{1,0:T(8,128)(2,1)} %param.3), kind=kOutput, calls=%fused_computation.2 | convolution fusion | flops 989327360 | bytes 23085056 | tf_op jit(solution)/shard_map/dot_general | solution.py:15
  257.5 177.6 %all-gather.7.cloned.1.call-done = bf16[1,256,30016]{2,1,0:T(8,128)(2,1)} async-done(((bf16[1,32,30016]{2,1,0:T(8,128)(2,1)}), bf16[1,256,30016]{2,1,0:T(8,128)(2,1)}) %all-gather.7.cloned.1.call-update) | async-done | bytes 15368208 | tf_op jit(solution)/shard_map/all_gather | solution.py:36
  435.0 11.2 %fusion.11 = bf16[64,256]{1,0:T(8,128)(2,1)S(1)} fusion(bf16[64,30016]{1,0:T(8,128)(2,1)} %fusion, bf16[1,256,30016]{2,1,0:T(8,128)(2,1)} %all-gather.7.cloned.1.call-done), kind=kOutput, calls=%fused_computation.11 | convolution fusion | flops 983580672 | bytes 19243008 | tf_op jit(solution)/shard_map/dot_general | solution.py:22
  446.3 10.4 %psum.15 = bf16[64,256]{1,0:T(8,128)(2,1)S(1)} all-reduce(bf16[64,256]{1,0:T(8,128)(2,1)S(1)} %fusion.11), channel_id=1, replica_groups=mesh['prow'=4,'pcol'=8] {'prow'}, use_global_device_ids=true, to_apply=%region_1.0 | all-reduce | flops 16384 | bytes 65536 | tf_op jit(solution)/shard_map/psum | solution.py:29
  456.6 0.3 convolution_convert_fusion
  456.9 8.7 %fusion.1 = bf16[64,30016]{1,0:T(8,128)(2,1)S(1)} fusion(bf16[64,256]{1,0:T(8,128)(2,1)S(1)} %convolution_convert_fusion, bf16[1,256,30016]{2,1,0:T(8,128)(2,1)} %all-gather.7.cloned.1.call-done, bf16[64,30016]{1,0:T(8,128)(2,1)} %fusion), kind=kOutput, calls=%fused_computation.3 | convolution fusion | flops 989327360 | bytes 23085056 | tf_op jit(solution)/shard_map/dot_general | solution.py:15
  465.6 47.1 %all_to_all.16 = bf16[4,16,30016]{2,1,0:T(8,128)(2,1)S(1)} all-to-all(bf16[4,16,30016]{2,1,0:T(8,128)(2,1)S(1)} %bitcast.28), channel_id=1, replica_groups=mesh['prow'=4,'pcol'=8] {'prow'}, dimensions={0} | all-to-all | bytes 7684096 | tf_op jit(solution)/shard_map/all_to_all | solution.py:38
  512.7 3.3 copy.4
  516.0 6.2 %broadcast_in_dim.3 = bf16[1,16,120064]{2,1,0:T(8,128)(2,1)} reshape(bf16[16,4,30016]{2,1,0:T(4,128)(2,1)} %copy.4) | data formatting | bytes 7684096 | tf_op jit(solution)/shard_map/broadcast_in_dim | solution.py:39
Async XLA Ops:
  6.5 217.6 %all-gather.5.cloned.1.call-start = ((), (), s32[]{:S(2)}) async-start(), calls=%async_computation.1 | async-start | bytes 17326080 | tf_op jit(solution)/shard_map/all_gather | solution.py:36
  10.8 424.2 %all-gather.7.cloned.1.call-start = ((), (), s32[]{:S(2)}) async-start(), calls=%async_computation.2 | async-start | bytes 17326080 | tf_op jit(solution)/shard_map/all_gather | solution.py:36
  11.6 235.0 %copy-start = (f32[2,256,256]{2,1,0:T(8,128)S(1)}, f32[2,256,256]{2,1,0:T(8,128)}, u32[]{:S(2)}) copy-start(f32[2,256,256]{2,1,0:T(8,128)} %param.5) | copy-start | bytes 1572868
Sparse Core Ops, SparseCore 0:
  10.9 213.1 all-gather.4
  226.3 208.6 all-gather.6
where the time goes:
time: 529 us
  waiting for transfers between devices  391 us (74%)
  blocking collectives  68.6 us (13%)
  matrix products  42.3 us (8%)
  local copies, waits for them, and re-layouts  13.8 us (3%)
  between operations  13.5 us (3%)
    all_gather x2, waiting for transfers between devices, body(): single = lax.all_gather(reflectors[number], 'pcol', axis=0, tiled=True)  390 us
    all_to_all x1, blocking collectives, body(): lax.all_to_all(current, 'prow', split_axis=0, concat_axis=1, tiled=True)  47.1 us
    dot_general x2, matrix products, partial_products(): lax.dot_general(current, panel, (((1,), (1,)), ((), ())), preferred_eleme...  22.5 us
    psum x2, blocking collectives, apply_panel(): lax.psum(partial_sum.astype(jnp.bfloat16), 'prow').astype(jnp.float32)  21.5 us
    dot_general x2, matrix products, finish_panel(): jnp.dot(scaled, panel, preferred_element_type=jnp.float32)  19.3 us
  transfers between devices with their start and end apart: 2, of which 2 were waited for; matrix products, arithmetic and copies ran while one was open for 4% of the time, Pallas kernels for 0%

commit v1 on v0

--- a/solution.py
+++ b/solution.py
@@ -33,7 +33,14 @@
 def body(vectors, reflectors, panel_factor):
     current = vectors
     for number in range(reflectors.shape[0]):
-        single = lax.all_gather(reflectors[number], "pcol", axis=0, tiled=True)
+        ring = [reflectors[number]]
+        for hop in range(7):
+            ring.append(lax.ppermute(ring[-1], "pcol", [(dev, (dev + 1) % 8) for dev in range(8)]))
+        single = jnp.roll(
+            jnp.concatenate(ring[::-1], axis=0),
+            (lax.axis_index("pcol") + 1) * ring[0].shape[0],
+            axis=0,
+        )
         current = apply_panel(current, single, panel_factor[number])
     owned_rows = lax.all_to_all(current, "prow", split_axis=0, concat_axis=1, tiled=True)
     return owned_rows[None]

time: 529 us -> 736 us (1.39)
  waiting for transfers between devices: 391 us -> 568 us
  local copies, waits for them, and re-layouts: 13.8 us -> 43.6 us
  between operations: 13.5 us -> 0.2 us
  matrix products: 42.3 us -> 51 us
    ppermute x0 -> x14, waiting for transfers between devices: none -> 568 us  [body(): lax.ppermute(ring[-1], 'pcol', [(dev, (dev + 1) % 8) for dev in range(8)])]
    all_gather x2 -> x0, waiting for transfers between devices: 390 us -> none  [body(): single = lax.all_gather(reflectors[number], 'pcol', axis=0, tiled=True)]
    unnamed x2 -> x48, local copies, waits for them, and re-layouts: 0.01 us -> 30.2 us
    dot_general x2, matrix products: 19.3 us -> 29 us  [finish_panel(): jnp.dot(scaled, panel, preferred_element_type=jnp.float32)]
  transfers between devices with their start and end apart: 2 -> 14, of which waited for: 2 -> 14; matrix products, arithmetic and copies ran while one was open for 4% -> 1% of each run, Pallas kernels for 0% -> 0%
where the time goes in v1:
time: 736 us
  waiting for transfers between devices  568 us (77%)
  blocking collectives  68.6 us (9%)
  matrix products  51 us (7%)
  local copies, waits for them, and re-layouts  43.6 us (6%)
    ppermute x14, waiting for transfers between devices, body(): lax.ppermute(ring[-1], 'pcol', [(dev, (dev + 1) % 8) for dev in range(8)])  568 us
    all_to_all x1, blocking collectives, body(): lax.all_to_all(current, 'prow', split_axis=0, concat_axis=1, tiled=True)  47 us
    unnamed x48, local copies, waits for them, and re-layouts  30.2 us
    dot_general x2, matrix products, finish_panel(): jnp.dot(scaled, panel, preferred_element_type=jnp.float32)  29 us
    psum x2, blocking collectives, apply_panel(): lax.psum(partial_sum.astype(jnp.bfloat16), 'prow').astype(jnp.float32)  21.7 us
    dot_general x2, matrix products, partial_products(): lax.dot_general(current, panel, (((1,), (1,)), ((), ())), preferred_eleme...  21.4 us
  transfers between devices with their start and end apart: 14, of which 14 were waited for; matrix products, arithmetic and copies ran while one was open for 1% of the time, Pallas kernels for 0%

profile of v1, /device:TPU:0, one launch (start us, length us, event | category | flops | bytes accessed | tf_op | source)
XLA Modules:
  0.0 735.7 jit_solution(15256260329332660349)
XLA Ops:
  0.0 2.4 slice_bitcast_fusion
  2.4 3.0 collective-permute-start
  6.9 44.3 %collective-permute-done = bf16[32,30016]{1,0:T(8,128)(2,1)S(1)} collective-permute-done((bf16[32,30016]{1,0:T(8,128)(2,1)S(1)}, bf16[32,30016]{1,0:T(8,128)(2,1)S(1)}, u32[]{:S(2)}, u32[]{:S(2)}) %collective-permute-start) | collective-permute-done | bytes 1921056 | tf_op jit(solution)/shard_map/ppermute | solution.py:38
  51.2 41.2 %collective-permute-done.7 = bf16[32,30016]{1,0:T(8,128)(2,1)S(1)} collective-permute-done((bf16[32,30016]{1,0:T(8,128)(2,1)S(1)}, bf16[32,30016]{1,0:T(8,128)(2,1)S(1)}, u32[]{:S(2)}, u32[]{:S(2)}) %collective-permute-start.7) | collective-permute-done | bytes 1921056 | tf_op jit(solution)/shard_map/ppermute | solution.py:38
  92.5 41.3 %collective-permute-done.1 = bf16[32,30016]{1,0:T(8,128)(2,1)S(1)} collective-permute-done((bf16[32,30016]{1,0:T(8,128)(2,1)S(1)}, bf16[32,30016]{1,0:T(8,128)(2,1)S(1)}, u32[]{:S(2)}, u32[]{:S(2)}) %collective-permute-start.1) | collective-permute-done | bytes 1921056 | tf_op jit(solution)/shard_map/ppermute | solution.py:38
  133.7 41.2 %collective-permute-done.8 = bf16[32,30016]{1,0:T(8,128)(2,1)S(1)} collective-permute-done((bf16[32,30016]{1,0:T(8,128)(2,1)S(1)}, bf16[32,30016]{1,0:T(8,128)(2,1)S(1)}, u32[]{:S(2)}, u32[]{:S(2)}) %collective-permute-start.8) | collective-permute-done | bytes 1921056 | tf_op jit(solution)/shard_map/ppermute | solution.py:38
  176.2 40.0 %collective-permute-done.2 = bf16[32,30016]{1,0:T(8,128)(2,1)S(1)} collective-permute-done((bf16[32,30016]{1,0:T(8,128)(2,1)S(1)}, bf16[32,30016]{1,0:T(8,128)(2,1)S(1)}, u32[]{:S(2)}, u32[]{:S(2)}) %collective-permute-start.2) | collective-permute-done | bytes 1921056 | tf_op jit(solution)/shard_map/ppermute | solution.py:38
  216.2 41.2 %collective-permute-done.9 = bf16[32,30016]{1,0:T(8,128)(2,1)S(1)} collective-permute-done((bf16[32,30016]{1,0:T(8,128)(2,1)S(1)}, bf16[32,30016]{1,0:T(8,128)(2,1)S(1)}, u32[]{:S(2)}, u32[]{:S(2)}) %collective-permute-start.9) | collective-permute-done | bytes 1921056 | tf_op jit(solution)/shard_map/ppermute | solution.py:38
  258.8 40.0 %collective-permute-done.3 = bf16[32,30016]{1,0:T(8,128)(2,1)S(1)} collective-permute-done((bf16[32,30016]{1,0:T(8,128)(2,1)S(1)}, bf16[32,30016]{1,0:T(8,128)(2,1)S(1)}, u32[]{:S(2)}, u32[]{:S(2)}) %collective-permute-start.3) | collective-permute-done | bytes 1921056 | tf_op jit(solution)/shard_map/ppermute | solution.py:38
  298.7 41.2 %collective-permute-done.10 = bf16[32,30016]{1,0:T(8,128)(2,1)S(1)} collective-permute-done((bf16[32,30016]{1,0:T(8,128)(2,1)S(1)}, bf16[32,30016]{1,0:T(8,128)(2,1)S(1)}, u32[]{:S(2)}, u32[]{:S(2)}) %collective-permute-start.10) | collective-permute-done | bytes 1921056 | tf_op jit(solution)/shard_map/ppermute | solution.py:38
  341.3 40.0 %collective-permute-done.4 = bf16[32,30016]{1,0:T(8,128)(2,1)S(1)} collective-permute-done((bf16[32,30016]{1,0:T(8,128)(2,1)S(1)}, bf16[32,30016]{1,0:T(8,128)(2,1)S(1)}, u32[]{:S(2)}, u32[]{:S(2)}) %collective-permute-start.4) | collective-permute-done | bytes 1921056 | tf_op jit(solution)/shard_map/ppermute | solution.py:38
  381.3 41.4 %collective-permute-done.11 = bf16[32,30016]{1,0:T(8,128)(2,1)} collective-permute-done((bf16[32,30016]{1,0:T(8,128)(2,1)S(1)}, bf16[32,30016]{1,0:T(8,128)(2,1)}, u32[]{:S(2)}, u32[]{:S(2)}) %collective-permute-start.11) | collective-permute-done | bytes 1921056 | tf_op jit(solution)/shard_map/ppermute | solution.py:38
  422.6 41.2 %collective-permute-done.5 = bf16[32,30016]{1,0:T(8,128)(2,1)} collective-permute-done((bf16[32,30016]{1,0:T(8,128)(2,1)S(1)}, bf16[32,30016]{1,0:T(8,128)(2,1)}, u32[]{:S(2)}, u32[]{:S(2)}) %collective-permute-start.5) | collective-permute-done | bytes 1921056 | tf_op jit(solution)/shard_map/ppermute | solution.py:38
  463.9 41.2 %collective-permute-done.12 = bf16[32,30016]{1,0:T(8,128)(2,1)} collective-permute-done((bf16[32,30016]{1,0:T(8,128)(2,1)}, bf16[32,30016]{1,0:T(8,128)(2,1)}, u32[]{:S(2)}, u32[]{:S(2)}) %collective-permute-start.12) | collective-permute-done | bytes 1921056 | tf_op jit(solution)/shard_map/ppermute | solution.py:38
  505.1 41.3 %collective-permute-done.6 = bf16[32,30016]{1,0:T(8,128)(2,1)} collective-permute-done((bf16[32,30016]{1,0:T(8,128)(2,1)}, bf16[32,30016]{1,0:T(8,128)(2,1)}, u32[]{:S(2)}, u32[]{:S(2)}) %collective-permute-start.6) | collective-permute-done | bytes 1921056 | tf_op jit(solution)/shard_map/ppermute | solution.py:38
  546.4 1.7 constant_dynamic-update-slice_fusion.7
  548.0 1.8 constant_dynamic-update-slice_fusion.6
  549.8 1.9 constant_dynamic-update-slice_fusion.5
  551.8 1.9 constant_dynamic-update-slice_fusion.4
  554.5 32.2 %collective-permute-done.13 = bf16[32,30016]{1,0:T(8,128)(2,1)S(1)} collective-permute-done((bf16[32,30016]{1,0:T(8,128)(2,1)}, bf16[32,30016]{1,0:T(8,128)(2,1)S(1)}, u32[]{:S(2)}, u32[]{:S(2)}) %collective-permute-start.13) | collective-permute-done | bytes 1921056 | tf_op jit(solution)/shard_map/ppermute | solution.py:38
  588.1 2.9 constant_dynamic-update-slice_fusion.14
  591.0 2.9 constant_dynamic-update-slice_fusion.13
  601.2 5.4 copy-done.16
  606.6 10.0 %fusion.4 = bf16[64,256]{0,1:T(8,128)(2,1)S(1)} fusion(bf16[64,30016]{1,0:T(8,128)(2,1)} %param.5, s32[]{:T(128)S(6)} %select_n.13, bf16[256,30016]{1,0:T(8,128)(2,1)} %copy-done.16), kind=kOutput, calls=%fused_computation.13 | convolution fusion | flops 1014317056 | bytes 19243012 | tf_op jit(solution)/shard_map/dot_general | solution.py:22
  616.6 10.9 %psum.14 = bf16[64,256]{0,1:T(8,128)(2,1)S(1)} all-reduce(bf16[64,256]{0,1:T(8,128)(2,1)S(1)} %fusion.4), channel_id=1, replica_groups=mesh['prow'=4,'pcol'=8] {'prow'}, use_global_device_ids=true, to_apply=%region_0.2 | all-reduce | flops 16384 | bytes 65536 | tf_op jit(solution)/shard_map/psum | solution.py:29
  627.7 15.1 %fusion = bf16[64,30016]{1,0:T(8,128)(2,1)} fusion(bf16[64,256]{1,0:T(8,128)(2,1)S(1)} %convolution_convert_fusion.3, bf16[64,30016]{1,0:T(8,128)(2,1)} %param.5, s32[]{:T(128)S(6)} %select_n.13, bf16[256,30016]{1,0:T(8,128)(2,1)} %copy-done.16), kind=kOutput, calls=%fused_computation.2 | convolution fusion | flops 1020063744 | bytes 23085060 | tf_op jit(solution)/shard_map/dot_general | solution.py:15
  642.9 11.5 %convolution_convert_fusion.1 = bf16[64,256]{1,0:T(8,128)(2,1)S(1)} fusion(bf16[64,30016]{1,0:T(8,128)(2,1)} %fusion, s32[]{:T(128)S(6)} %select_n.13, bf16[256,30016]{1,0:T(8,128)(2,1)} %get-tuple-element.6), kind=kOutput, calls=%fused_computation.14 | convolution fusion | flops 1014317056 | bytes 19243012 | tf_op jit(solution)/shard_map/dot_general | solution.py:22
  654.3 10.8 %psum.15 = bf16[64,256]{1,0:T(8,128)(2,1)S(1)} all-reduce(bf16[64,256]{1,0:T(8,128)(2,1)S(1)} %convolution_convert_fusion.1), channel_id=1, replica_groups=mesh['prow'=4,'pcol'=8] {'prow'}, use_global_device_ids=true, to_apply=%region_1.3 | all-reduce | flops 16384 | bytes 65536 | tf_op jit(solution)/shard_map/psum | solution.py:29
  665.4 13.8 %fusion.1 = bf16[64,30016]{1,0:T(8,128)(2,1)S(1)} fusion(bf16[64,256]{1,0:T(8,128)(2,1)S(1)} %convolution_convert_fusion.2, bf16[64,30016]{1,0:T(8,128)(2,1)} %fusion, s32[]{:T(128)S(6)} %select_n.13, bf16[256,30016]{1,0:T(8,128)(2,1)} %get-tuple-element.6), kind=kOutput, calls=%fused_computation.3 | convolution fusion | flops 1020063744 | bytes 23085060 | tf_op jit(solution)/shard_map/dot_general | solution.py:15
  679.3 47.0 %all_to_all.16 = bf16[4,16,30016]{2,1,0:T(8,128)(2,1)S(1)} all-to-all(bf16[4,16,30016]{2,1,0:T(8,128)(2,1)S(1)} %bitcast.25), channel_id=1, replica_groups=mesh['prow'=4,'pcol'=8] {'prow'}, dimensions={0} | all-to-all | bytes 7684096 | tf_op jit(solution)/shard_map/all_to_all | solution.py:45
  726.2 3.3 copy.4
  729.6 6.2 broadcast_in_dim.3
  (57 shorter events, 15.3 us)
Async XLA Ops:
  2.4 48.9 %collective-permute-start = (bf16[32,30016]{1,0:T(8,128)(2,1)S(1)}, bf16[32,30016]{1,0:T(8,128)(2,1)S(1)}, u32[]{:S(2)}, u32[]{:S(2)}) collective-permute-start(bf16[32,30016]{1,0:T(8,128)(2,1)S(1)} %get-tuple-element.9), channel_id=1, source_target_pairs={{0,1},{1,2},{2,3},{3,4},{4,5},{5,6},{6,7},{7,0},{8,9},{9,10},{10,1... | collective-permute-start | bytes 5763080 | tf_op jit(solution)/shard_map/ppermute | solution.py:38
  5.4 87.1 %collective-permute-start.7 = (bf16[32,30016]{1,0:T(8,128)(2,1)S(1)}, bf16[32,30016]{1,0:T(8,128)(2,1)S(1)}, u32[]{:S(2)}, u32[]{:S(2)}) collective-permute-start(bf16[32,30016]{1,0:T(8,128)(2,1)S(1)} %get-tuple-element.8), channel_id=1, source_target_pairs={{0,1},{1,2},{2,3},{3,4},{4,5},{5,6},{6,7},{7,0},{8,9},{9,10},{10,1... | collective-permute-start | bytes 5763080 | tf_op jit(solution)/shard_map/ppermute | solution.py:38
  51.2 123.8 %copy-start.1 = (bf16[32,30016]{1,0:T(8,128)(2,1)}, bf16[32,30016]{1,0:T(8,128)(2,1)S(1)}, u32[]{:S(2)}) copy-start(bf16[32,30016]{1,0:T(8,128)(2,1)S(1)} %collective-permute-done) | copy-start | bytes 5763076
  51.2 82.5 %collective-permute-start.1 = (bf16[32,30016]{1,0:T(8,128)(2,1)S(1)}, bf16[32,30016]{1,0:T(8,128)(2,1)S(1)}, u32[]{:S(2)}, u32[]{:S(2)}) collective-permute-start(bf16[32,30016]{1,0:T(8,128)(2,1)S(1)} %collective-permute-done), channel_id=1, source_target_pairs={{0,1},{1,2},{2,3},{3,4},{4,5},{5,6},{6,7},{7,0},{8,9},{9,10},{10,1... | collective-permute-start | bytes 5763080 | tf_op jit(solution)/shard_map/ppermute | solution.py:38
  92.5 82.5 %collective-permute-start.8 = (bf16[32,30016]{1,0:T(8,128)(2,1)S(1)}, bf16[32,30016]{1,0:T(8,128)(2,1)S(1)}, u32[]{:S(2)}, u32[]{:S(2)}) collective-permute-start(bf16[32,30016]{1,0:T(8,128)(2,1)S(1)} %collective-permute-done.7), channel_id=1, source_target_pairs={{0,1},{1,2},{2,3},{3,4},{4,5},{5,6},{6,7},{7,0},{8,9},{9,10},{10,1... | collective-permute-start | bytes 5763080 | tf_op jit(solution)/shard_map/ppermute | solution.py:38
  133.7 123.8 %copy-start.5 = (bf16[32,30016]{1,0:T(8,128)(2,1)}, bf16[32,30016]{1,0:T(8,128)(2,1)S(1)}, u32[]{:S(2)}) copy-start(bf16[32,30016]{1,0:T(8,128)(2,1)S(1)} %collective-permute-done.1) | copy-start | bytes 5763076
  133.7 82.5 %collective-permute-start.2 = (bf16[32,30016]{1,0:T(8,128)(2,1)S(1)}, bf16[32,30016]{1,0:T(8,128)(2,1)S(1)}, u32[]{:S(2)}, u32[]{:S(2)}) collective-permute-start(bf16[32,30016]{1,0:T(8,128)(2,1)S(1)} %collective-permute-done.1), channel_id=1, source_target_pairs={{0,1},{1,2},{2,3},{3,4},{4,5},{5,6},{6,7},{7,0},{8,9},{9,10},{10,1... | collective-permute-start | bytes 5763080 | tf_op jit(solution)/shard_map/ppermute | solution.py:38
  175.0 1.3 copy-start.3
  175.0 82.5 %collective-permute-start.9 = (bf16[32,30016]{1,0:T(8,128)(2,1)S(1)}, bf16[32,30016]{1,0:T(8,128)(2,1)S(1)}, u32[]{:S(2)}, u32[]{:S(2)}) collective-permute-start(bf16[32,30016]{1,0:T(8,128)(2,1)S(1)} %collective-permute-done.8), channel_id=1, source_target_pairs={{0,1},{1,2},{2,3},{3,4},{4,5},{5,6},{6,7},{7,0},{8,9},{9,10},{10,1... | collective-permute-start | bytes 5763080 | tf_op jit(solution)/shard_map/ppermute | solution.py:38
  216.2 123.8 %copy-start.9 = (bf16[32,30016]{1,0:T(8,128)(2,1)}, bf16[32,30016]{1,0:T(8,128)(2,1)S(1)}, u32[]{:S(2)}) copy-start(bf16[32,30016]{1,0:T(8,128)(2,1)S(1)} %collective-permute-done.2) | copy-start | bytes 5763076
  216.2 82.5 %collective-permute-start.3 = (bf16[32,30016]{1,0:T(8,128)(2,1)S(1)}, bf16[32,30016]{1,0:T(8,128)(2,1)S(1)}, u32[]{:S(2)}, u32[]{:S(2)}) collective-permute-start(bf16[32,30016]{1,0:T(8,128)(2,1)S(1)} %collective-permute-done.2), channel_id=1, source_target_pairs={{0,1},{1,2},{2,3},{3,4},{4,5},{5,6},{6,7},{7,0},{8,9},{9,10},{10,1... | collective-permute-start | bytes 5763080 | tf_op jit(solution)/shard_map/ppermute | solution.py:38
  257.5 1.3 copy-start.7
  257.5 82.5 %collective-permute-start.10 = (bf16[32,30016]{1,0:T(8,128)(2,1)S(1)}, bf16[32,30016]{1,0:T(8,128)(2,1)S(1)}, u32[]{:S(2)}, u32[]{:S(2)}) collective-permute-start(bf16[32,30016]{1,0:T(8,128)(2,1)S(1)} %collective-permute-done.9), channel_id=1, source_target_pairs={{0,1},{1,2},{2,3},{3,4},{4,5},{5,6},{6,7},{7,0},{8,9},{9,10},{10,1... | collective-permute-start | bytes 5763080 | tf_op jit(solution)/shard_map/ppermute | solution.py:38
  298.7 123.9 %copy-start.13 = (bf16[32,30016]{1,0:T(8,128)(2,1)}, bf16[32,30016]{1,0:T(8,128)(2,1)S(1)}, u32[]{:S(2)}) copy-start(bf16[32,30016]{1,0:T(8,128)(2,1)S(1)} %collective-permute-done.3) | copy-start | bytes 5763076
  298.7 82.5 %collective-permute-start.4 = (bf16[32,30016]{1,0:T(8,128)(2,1)S(1)}, bf16[32,30016]{1,0:T(8,128)(2,1)S(1)}, u32[]{:S(2)}, u32[]{:S(2)}) collective-permute-start(bf16[32,30016]{1,0:T(8,128)(2,1)S(1)} %collective-permute-done.3), channel_id=1, source_target_pairs={{0,1},{1,2},{2,3},{3,4},{4,5},{5,6},{6,7},{7,0},{8,9},{9,10},{10,1... | collective-permute-start | bytes 5763080 | tf_op jit(solution)/shard_map/ppermute | solution.py:38
  340.0 1.3 copy-start.11
  340.0 82.6 %collective-permute-start.11 = (bf16[32,30016]{1,0:T(8,128)(2,1)S(1)}, bf16[32,30016]{1,0:T(8,128)(2,1)}, u32[]{:S(2)}, u32[]{:S(2)}) collective-permute-start(bf16[32,30016]{1,0:T(8,128)(2,1)S(1)} %collective-permute-done.10), channel_id=1, source_target_pairs={{0,1},{1,2},{2,3},{3,4},{4,5},{5,6},{6,7},{7,0},{8,9},{9,10},{10,1... | collective-permute-start | bytes 5763080 | tf_op jit(solution)/shard_map/ppermute | solution.py:38
  381.3 41.4 %copy-start.14 = (bf16[32,30016]{1,0:T(8,128)(2,1)}, bf16[32,30016]{1,0:T(8,128)(2,1)S(1)}, u32[]{:S(2)}) copy-start(bf16[32,30016]{1,0:T(8,128)(2,1)S(1)} %collective-permute-done.4) | copy-start | bytes 5763076
  381.3 82.6 %collective-permute-start.5 = (bf16[32,30016]{1,0:T(8,128)(2,1)S(1)}, bf16[32,30016]{1,0:T(8,128)(2,1)}, u32[]{:S(2)}, u32[]{:S(2)}) collective-permute-start(bf16[32,30016]{1,0:T(8,128)(2,1)S(1)} %collective-permute-done.4), channel_id=1, source_target_pairs={{0,1},{1,2},{2,3},{3,4},{4,5},{5,6},{6,7},{7,0},{8,9},{9,10},{10,1... | collective-permute-start | bytes 5763080 | tf_op jit(solution)/shard_map/ppermute | solution.py:38
  422.6 82.5 %collective-permute-start.12 = (bf16[32,30016]{1,0:T(8,128)(2,1)}, bf16[32,30016]{1,0:T(8,128)(2,1)}, u32[]{:S(2)}, u32[]{:S(2)}) collective-permute-start(bf16[32,30016]{1,0:T(8,128)(2,1)} %collective-permute-done.11), channel_id=1, source_target_pairs={{0,1},{1,2},{2,3},{3,4},{4,5},{5,6},{6,7},{7,0},{8,9},{9,10},{10,1... | collective-permute-start | bytes 5763080 | tf_op jit(solution)/shard_map/ppermute | solution.py:38
  463.9 82.5 %collective-permute-start.6 = (bf16[32,30016]{1,0:T(8,128)(2,1)}, bf16[32,30016]{1,0:T(8,128)(2,1)}, u32[]{:S(2)}, u32[]{:S(2)}) collective-permute-start(bf16[32,30016]{1,0:T(8,128)(2,1)} %collective-permute-done.5), channel_id=1, source_target_pairs={{0,1},{1,2},{2,3},{3,4},{4,5},{5,6},{6,7},{7,0},{8,9},{9,10},{10,1... | collective-permute-start | bytes 5763080 | tf_op jit(solution)/shard_map/ppermute | solution.py:38
  463.9 89.8 %copy-start.10 = (bf16[32,30016]{1,0:T(8,128)(2,1)S(1)}, bf16[32,30016]{1,0:T(8,128)(2,1)}, u32[]{:S(2)}) copy-start(bf16[32,30016]{1,0:T(8,128)(2,1)} %copy-done.9) | copy-start | bytes 5763076
  463.9 90.1 %copy-start.6 = (bf16[32,30016]{1,0:T(8,128)(2,1)S(1)}, bf16[32,30016]{1,0:T(8,128)(2,1)}, u32[]{:S(2)}) copy-start(bf16[32,30016]{1,0:T(8,128)(2,1)} %copy-done.5) | copy-start | bytes 5763076
  463.9 90.3 %copy-start.2 = (bf16[32,30016]{1,0:T(8,128)(2,1)S(1)}, bf16[32,30016]{1,0:T(8,128)(2,1)}, u32[]{:S(2)}) copy-start(bf16[32,30016]{1,0:T(8,128)(2,1)} %copy-done.1) | copy-start | bytes 5763076
  505.1 81.6 %collective-permute-start.13 = (bf16[32,30016]{1,0:T(8,128)(2,1)}, bf16[32,30016]{1,0:T(8,128)(2,1)S(1)}, u32[]{:S(2)}, u32[]{:S(2)}) collective-permute-start(bf16[32,30016]{1,0:T(8,128)(2,1)} %collective-permute-done.12), channel_id=1, source_target_pairs={{0,1},{1,2},{2,3},{3,4},{4,5},{5,6},{6,7},{7,0},{8,9},{9,10},{10,1... | collective-permute-start | bytes 5763080 | tf_op jit(solution)/shard_map/ppermute | solution.py:38
  549.8 44.1 %copy-start.12 = (bf16[32,30016]{1,0:T(8,128)(2,1)S(1)}, bf16[32,30016]{1,0:T(8,128)(2,1)}, u32[]{:S(2)}) copy-start(bf16[32,30016]{1,0:T(8,128)(2,1)} %copy-done.11) | copy-start | bytes 5763076
  551.7 43.6 %copy-start.8 = (bf16[32,30016]{1,0:T(8,128)(2,1)S(1)}, bf16[32,30016]{1,0:T(8,128)(2,1)}, u32[]{:S(2)}) copy-start(bf16[32,30016]{1,0:T(8,128)(2,1)} %copy-done.7) | copy-start | bytes 5763076
  553.7 43.1 %copy-start.4 = (bf16[32,30016]{1,0:T(8,128)(2,1)S(1)}, bf16[32,30016]{1,0:T(8,128)(2,1)}, u32[]{:S(2)}) copy-start(bf16[32,30016]{1,0:T(8,128)(2,1)} %copy-done.3) | copy-start | bytes 5763076
  554.2 45.4 %copy-start = (bf16[2,32,30016]{2,1,0:T(8,128)(2,1)S(1)}, bf16[2,32,30016]{2,1,0:T(8,128)(2,1)}, u32[]{:S(2)}) copy-start(bf16[2,32,30016]{2,1,0:T(8,128)(2,1)} %param.6) | copy-start | bytes 11526148
  601.2 5.4 copy-start.16
  606.6 20.8 %copy-start.15 = (f32[2,256,256]{2,1,0:T(8,128)S(1)}, f32[2,256,256]{2,1,0:T(8,128)}, u32[]{:S(2)}) copy-start(f32[2,256,256]{2,1,0:T(8,128)} %param.7) | copy-start | bytes 1572868
